TPU v7x, 128 devices: a whole 4x4x4 slice. The times are simulated.
128 devices in a mesh: dp: 1, tp: 2 (over core), fsdp: 64 (over z, y, x).
Axes of the slice: x: 4, y: 4, z: 4, core: 2. Of those that a mesh axis runs over, the one named last changes fastest.
Arguments:
- tokens: int32 [128, 2048], P(('dp', 'fsdp'))
- out_grad: bfloat16 [128, 2048, 1024], P(('dp', 'fsdp'))
- head_grad: float32 [32128, 1024], P(('dp', 'tp'), 'fsdp')
- master_w: float32 [32128, 1024], P(('dp', 'tp'), 'fsdp')
- moment_m: float32 [32128, 1024], P(('dp', 'tp'), 'fsdp')
- moment_v: float32 [32128, 1024], P(('dp', 'tp'), 'fsdp')
- learn_rate: float32 [], replicated
- clip_scale: float32 [], replicated
Outputs:
- output 1: float32 [32128, 1024], P(('dp', 'tp'), 'fsdp')
- output 2: float32 [32128, 1024], P(('dp', 'tp'), 'fsdp')
- output 3: float32 [32128, 1024], P(('dp', 'tp'), 'fsdp')
- output 4: bfloat16 [32128, 1024], P(('dp', 'tp'), 'fsdp')
All inputs are finite; a program needn't handle non-finite values.
Results may differ from a plain program's by a relative error of at most 0.001.
Values sent between devices are 32-bit elements.
A program may use at most 1 GiB of HBM per device.

v0:
```python
import functools

import jax
import jax.numpy as jnp
from jax import lax
from jax.experimental import pallas as pl
from jax.experimental.pallas import tpu as pltpu
from jax.sharding import PartitionSpec as P

OPT_STEP = 20
F32, BF16, I32 = jnp.float32, jnp.bfloat16, jnp.int32
CAP = (480, 352, 208)
KW = 512
STRIDES = ((1, 16), (4, 1), (16, 4))
VLIM = 20 << 20
MESH = pl.DeviceIdType.MESH
ORDER = (2, 1, 3, 0)


def update_math(embed_grad, head_grad, master_w, moment_m, moment_v, learn_rate, clip_scale):
    beta_two = 1.0 - OPT_STEP ** -0.8
    grad_full = clip_scale * (embed_grad + head_grad)
    new_v = beta_two * moment_v + (1.0 - beta_two) * (grad_full * grad_full + 1e-30)
    new_m = 0.9 * moment_m + 0.1 * (grad_full / jnp.sqrt(new_v))
    new_w = master_w - learn_rate * new_m - learn_rate * learn_rate * master_w
    return new_w, new_m, new_v


def iota(shape, dim):
    return lax.broadcasted_iota(I32, shape, dim)


def onehot(cond):
    return jnp.where(cond, 1.0, 0.0).astype(BF16)


def dot_nt(a, b):
    return lax.dot_general(a, b, (((1,), (1,)), ((), ())), preferred_element_type=F32)


def dot_nn(a, b):
    return jnp.dot(a, b, preferred_element_type=F32)


def ranks(pres, group):
    rows = pres.shape[0]
    pres_b = pres.astype(BF16)
    before = onehot(iota((KW, KW), 0) < iota((KW, KW), 1))
    inner = dot_nn(pres_b, before)
    if group > 1:
        r, c = iota((rows, rows), 0), iota((rows, rows), 1)
        above = onehot((c < r) & (c // group == r // group))
        inner = inner + jnp.sum(dot_nn(above, pres_b), axis=1, keepdims=True)
    return inner.astype(I32)


def codes(pres, group, cap):
    rows = pres.shape[0]
    rank = ranks(pres, group)
    code = jnp.where((pres > 0.5) & (rank < cap), (iota((rows, KW), 0) // group) * cap + rank + 1, 0)
    over = jnp.where((pres > 0.5) & (rank >= cap), 1.0, 0.0)
    return code, jnp.max(over)


def index_first(coords, tok_ref, slot_ref, tables):
    ids = tok_ref[...]
    tp, c1, c2, c3 = coords
    x, y, z = ids & 3, (ids >> 2) & 3, (ids >> 4) & 3
    d1 = x + (z - x) * tp
    d2 = y + (x - y) * tp
    d3 = z + (y - z) * tp
    q = (((d1 - c1) & 3) << 4) + (((d2 - c2) & 3) << 2) + ((d3 - c3) & 3)
    upper = ids >= 16064
    kk = jnp.where(upper, ids - 16064, ids) >> 6
    k = jnp.where(upper, 256, 0) + ((kk & 1) << 7) + (kk >> 1)
    n = ids.shape[1]
    hot_q = onehot(iota((64, n), 0) == q)
    hot_k = onehot(iota((KW, n), 0) == k)
    pres = jnp.minimum(dot_nt(hot_q, hot_k), 1.0)
    code, over = codes(pres, 16, CAP[0])
    both = jnp.concatenate([(code >> 5).astype(BF16), (code & 31).astype(BF16)], axis=0)
    found = dot_nn(both, hot_k)
    value = found[:64] * 32.0 + found[64:]
    slot_ref[...] = jnp.sum(jnp.where(iota((64, n), 0) == q, value, 0.0), axis=0, keepdims=True).astype(I32) - 1
    for o in range(4):
        tables[o] = pres[16 * o:16 * o + 16]
    return over


def gather_first(o, slot_ref, rows_ref, out_ref):
    cap, depth = out_ref.shape[0], 1024

    def step(n, first):
        at = pl.ds(pl.multiple_of(n * depth, depth), depth)
        hot = onehot(iota((cap, depth), 0) == slot_ref[:, at] - o * cap)
        part = dot_nn(hot, rows_ref[at, :])
        out_ref[...] = part if first else out_ref[...] + part

    step(0, True)
    lax.fori_loop(1, rows_ref.shape[0] // depth, lambda n, c: (step(n, False), c)[1], 0)


def index_next(group, cap_out, blocks, slot_ref, tables):
    blocks = [block[:4 * group] for block in blocks]
    merged = jnp.minimum(blocks[0] + blocks[1] + blocks[2] + blocks[3], 1.0)
    rows = merged.shape[0]
    code, over = codes(merged, group, cap_out)
    hi, lo = (code >> 5).astype(F32), (code & 31).astype(F32)
    lanes = iota((32, KW), 1)
    spread = onehot((lanes & 31) == iota((32, KW), 0))
    own_row = (iota((16, KW), 1) >> 5) == iota((16, KW), 0)
    for s, pres in enumerate(blocks):
        rank = jnp.where(pres > 0.5, ranks(pres, rows), -1)
        table = jnp.zeros((16, 64), F32)
        for r in range(rows):
            row = rank[r:r + 1]
            high = onehot(iota((16, KW), 0) == (row >> 5))
            low = iota((32, KW), 0) == (row & 31)
            low = jnp.concatenate([jnp.where(low, hi[r:r + 1], 0.0), jnp.where(low, lo[r:r + 1], 0.0)], axis=0)
            table = table + dot_nt(high, low.astype(BF16))
        table = table.astype(BF16)
        value = dot_nn(table[:, :32], spread) * 32.0 + dot_nn(table[:, 32:], spread)
        slot_ref[s:s + 1, :] = jnp.sum(jnp.where(own_row, value, 0.0), axis=0, keepdims=True).astype(I32) - 1
    tables[...] = jnp.zeros(tables.shape, F32)
    for o in range(4):
        tables[o, :group] = merged[group * o:group * o + group]
    return over


def split_rows(rows):
    high = jnp.clip(rows, -3.38e38, 3.38e38).astype(BF16)
    rest = rows - high.astype(F32)
    mid = rest.astype(BF16)
    return high, mid, (rest - mid.astype(F32)).astype(BF16)


def gather_next(o, slot_ref, blocks, out_ref):
    cap_out, cap_in = out_ref.shape[0], blocks[0].shape[0]
    hots = [onehot(iota((cap_out, cap_in), 0) == slot_ref[s:s + 1, :cap_in] - o * cap_out) for s in range(4)]

    def columns(n, carry):
        at = pl.ds(pl.multiple_of(n * 256, 256), 256)
        total = None
        for hot, rows in zip(hots, blocks):
            for piece in split_rows(rows[:, at]):
                part = dot_nn(hot, piece)
                total = part if total is None else total + part
        out_ref[:, at] = total
        return carry

    lax.fori_loop(0, out_ref.shape[1] // 256, columns, 0)


def dense_last(tables, blocks, flag, out_ref):
    total = None
    for pres_ref, rows in zip(tables, blocks):
        pres = pres_ref[...]
        rank = jnp.where(pres > 0.5, ranks(pres, 1), -1)[0:1]
        hot = onehot(iota((rows.shape[0], KW), 0) == rank)
        for piece in split_rows(rows[...].T):
            part = dot_nn(piece, hot)
            total = part if total is None else total + part
    total = jnp.where((iota(total.shape, 1) & 255) == 255, flag, total)
    for t in range(2):
        out_ref[t] = total[:, 256 * t:256 * t + 256].reshape(out_ref.shape[1:])


def assemble(tok_ref, rows_ref, recv_ref, half, slot1, slot2, slot3, tab1, tab2, tab3, rtab1, rtab2, rtab3, send1, send2, send3,
             recv1, recv2, recv3, own_over, peer_over, dense, half_sem, tab_out, tab_in, row_out, row_in, over_out, over_in, last_out, last_in):
    tp, me = lax.axis_index("tp"), lax.axis_index("fsdp")
    ring = []
    for low, high in STRIDES:
        stride = low + (high - low) * tp
        ring.append((stride, (me // stride) % 4))
    coords = (tp, *(at for _, at in ring))
    width = half.shape[1]
    side = me // 32
    same = 1 - (side + tp) % 2

    def neighbour(phase, offset):
        stride, at = ring[phase]
        return {"fsdp": me + stride * ((at + offset) % 4 - at)}

    barrier = pltpu.get_barrier_semaphore()

    def greet(device):
        pl.semaphore_signal(barrier, inc=1, device_id=device, device_id_type=MESH)

    for phase in range(3):
        for o in (1, 2, 3):
            greet(neighbour(phase, o))
    greet({"tp": 1 - tp})

    def greet_source(i, carry):
        greet({"fsdp": (me + i) % 64, "tp": side})
        return carry

    lax.fori_loop(1, 64, greet_source, 0)

    @pl.when(same == 0)
    def _():
        greet({"tp": side})

    load = pltpu.make_async_copy(rows_ref.at[:, pl.ds(pl.multiple_of(tp * width, width), width)], half, half_sem)
    load.start()
    over = index_first(coords, tok_ref, slot1, tab1)
    pl.semaphore_wait(barrier, 74 - same)

    def remote(src, dst, out, into, device):
        copy = pltpu.make_async_remote_copy(
            src_ref=src, dst_ref=dst, send_sem=out, recv_sem=into, device_id=device, device_id_type=MESH)
        copy.start()
        return copy

    def send_tables(phase, table, into):
        return [remote(table.at[o], into.at[o - 1], tab_out.at[3 * phase + o - 1], tab_in.at[3 * phase + o - 1], neighbour(phase, o))
                for o in (1, 2, 3)]

    def send_row(phase, o, rows, into):
        return remote(rows.at[o], into.at[o - 1], row_out.at[3 * phase + o - 1], row_in.at[3 * phase + o - 1], neighbour(phase, o))

    def wait(copies):
        for copy in copies:
            copy.wait()

    def beside(own, got):
        return [own.at[0], *(got.at[n] for n in range(3))]

    tables = send_tables(0, tab1, rtab1)
    load.wait()
    rows = []
    for o in ORDER:
        gather_first(o, slot1, half, send1.at[o])
        if o:
            rows.append(send_row(0, o, send1, recv1))

    wait(tables)
    over = jnp.maximum(over, index_next(4, CAP[1], beside(tab1, rtab1), slot2, tab2))
    tables = send_tables(1, tab2, rtab2)
    wait(tables)
    over = jnp.maximum(over, index_next(1, CAP[2], beside(tab2, rtab2), slot3, tab3))
    own_over[...] = jnp.full(own_over.shape, over, F32)
    tables = send_tables(2, tab3, rtab3)
    tables.append(remote(own_over, peer_over, over_out, over_in, {"tp": 1 - tp}))

    wait(rows)
    rows = []
    for o in ORDER:
        gather_next(o, slot2, beside(send1, recv1), send2.at[o])
        if o:
            rows.append(send_row(1, o, send2, recv2))
    wait(rows)
    rows = []
    for o in ORDER:
        gather_next(o, slot3, beside(send2, recv2), send3.at[o])
        if o:
            rows.append(send_row(2, o, send3, recv3))
    wait(tables)
    wait(rows)
    flag = jnp.maximum(own_over[0:1, 0:1], peer_over[0:1, 0:1])
    dense_last(beside(tab3, rtab3), beside(send3, recv3), flag, dense)

    def last(i, far):
        at = (me + i) % 32
        core = (tp + far) % 2
        return pltpu.make_async_remote_copy(
            src_ref=dense.at[core, at], dst_ref=recv_ref.at[me], send_sem=last_out.at[2 * i + far], recv_sem=last_in.at[me],
            device_id={"fsdp": 32 * tp + at, "tp": core}, device_id_type=MESH)

    def arrive(j):
        return pltpu.make_async_remote_copy(
            src_ref=dense.at[0, 0], dst_ref=recv_ref.at[j], send_sem=last_out.at[0], recv_sem=last_in.at[j],
            device_id={"tp": 1 - tp}, device_id_type=MESH)

    def start_pair(i, carry):
        last(i, 0).start()
        last(i, 1).start()
        return carry

    lax.fori_loop(1, 32, start_pair, 0)
    last(0, 1).start()

    @pl.when(same == 0)
    def _():
        last(0, 0).start()

    @pl.when(same == 1)
    def _():
        recv_ref[me] = dense[tp, me % 32]

    def wait_pair(i, carry):
        last(i, 0).wait_send()
        last(i, 1).wait_send()
        return carry

    def wait_arrival(i, carry):
        arrive((me + i) % 64).wait_recv()
        return carry

    lax.fori_loop(1, 64, wait_arrival, 0)
    lax.fori_loop(1, 32, wait_pair, 0)
    last(0, 1).wait_send()

    @pl.when(same == 0)
    def _():
        arrive(me).wait_recv()
        last(0, 0).wait_send()


def finish(scal_ref, recv_ref, head_ref, w_ref, m_ref, v_ref, w_out, m_out, v_out, b_out, grad):
    tiles = grad.shape[0]
    for c in range(16):
        both = jnp.concatenate([recv_ref[:, c, :128], recv_ref[:, c, 128:]], axis=0)
        grad[:, c, :] = both.T[:tiles]
    lr, clip = scal_ref[0], scal_ref[1]
    rows = head_ref.shape[1]
    for t in range(tiles):
        at = slice(128 * t, min(128 * t + 128, rows))
        width = at.stop - at.start
        new_w, new_m, new_v = update_math(grad[t, :, :width], head_ref[:, at], w_ref[:, at], m_ref[:, at], v_ref[:, at], lr, clip)
        w_out[:, at], m_out[:, at], v_out[:, at] = new_w, new_m, new_v
        b_out[:, at] = new_w.astype(BF16)


def shaped(*shape, dtype=F32):
    return jax.ShapeDtypeStruct(shape, dtype)


def dense_rows(ids_ref, rows_ref, out_ref):
    first = pl.program_id(0) * out_ref.shape[0]
    hot = onehot(iota((out_ref.shape[0], rows_ref.shape[0]), 0) + first == ids_ref[...])
    part = dot_nn(hot, rows_ref[...])

    @pl.when(pl.program_id(1) == 0)
    def _():
        out_ref[...] = part

    @pl.when(pl.program_id(1) > 0)
    def _():
        out_ref[...] += part


def solution(mesh):
    row_spec = P(("dp", "fsdp"), None)
    act_spec = P(("dp", "fsdp"), None, None)
    table_spec = P(("dp", "tp"), "fsdp")

    def dense_grad(ids, rows, shard_rows):
        n, width = rows.shape
        block, depth = 256, 1024
        tiles = -(-shard_rows // block)
        part = pl.pallas_call(
            dense_rows,
            grid=(tiles, n // depth),
            in_specs=[pl.BlockSpec((1, depth), lambda i, k: (0, k)), pl.BlockSpec((depth, width), lambda i, k: (k, 0))],
            out_specs=pl.BlockSpec((block, width), lambda i, k: (i, 0)),
            out_shape=shaped(tiles * block, width),
            compiler_params=pltpu.CompilerParams(vmem_limit_bytes=VLIM),
            name="dense_rows",
        )(ids - lax.axis_index("tp") * shard_rows, rows)
        part = part[:shard_rows].T.reshape(64, 16, shard_rows)
        return jnp.sum(lax.all_to_all(part, "fsdp", 0, 0, tiled=True), axis=0)

    def local_step(tokens, out_grad, head_grad, master_w, moment_m, moment_v, learn_rate, clip_scale):
        ids = tokens.reshape(1, -1)
        n = ids.shape[1]
        rows = out_grad.reshape(n, -1)
        width = rows.shape[1] // 2
        vm, dma = pltpu.VMEM, pltpu.SemaphoreType.DMA
        recv = pl.pallas_call(
            assemble,
            out_shape=shaped(64, 16, 256),
            in_specs=[pl.BlockSpec(memory_space=vm), pl.BlockSpec(memory_space=pl.ANY)],
            out_specs=pl.BlockSpec(memory_space=vm),
            scratch_shapes=[
                vm((n, width), BF16), vm((1, n), I32), vm((4, KW), I32), vm((4, KW), I32),
                vm((4, 16, KW), F32), vm((4, 8, KW), F32), vm((4, 8, KW), F32),
                vm((3, 16, KW), F32), vm((3, 8, KW), F32), vm((3, 8, KW), F32),
                *[vm((4, cap, width), F32) for cap in CAP],
                *[vm((3, cap, width), F32) for cap in CAP],
                vm((8, 128), F32), vm((8, 128), F32), vm((2, 32, 16, 256), F32),
                dma, dma((9,)), dma((9,)), dma((9,)), dma((9,)), dma, dma, dma((64,)), dma((64,)),
            ],
            compiler_params=pltpu.CompilerParams(vmem_limit_bytes=52 << 20, collective_id=0, has_side_effects=True),
            name="assemble",
        )(ids, rows)
        flag = jnp.max(recv[:, 0, 255]) > 0.5

        scal = jnp.stack([learn_rate, clip_scale])
        tables = (head_grad.T, master_w.T, moment_m.T, moment_v.T)
        shard_rows = master_w.shape[0]
        shard = (16, shard_rows)

        def fast(_):
            return pl.pallas_call(
                finish,
                out_shape=(shaped(*shard), shaped(*shard), shaped(*shard), shaped(*shard, dtype=BF16)),
                in_specs=[pl.BlockSpec(memory_space=pltpu.SMEM)] + [pl.BlockSpec(memory_space=pltpu.VMEM)] * 5,
                out_specs=tuple(pl.BlockSpec(memory_space=pltpu.VMEM) for _ in range(4)),
                scratch_shapes=[pltpu.VMEM(((shard_rows + 127) // 128, 16, 128), F32)],
                compiler_params=pltpu.CompilerParams(vmem_limit_bytes=VLIM),
                name="finish",
            )(scal, recv, *tables)

        def slow(_):
            grad = dense_grad(ids, rows, shard_rows)
            new_w, new_m, new_v = update_math(grad, *tables, learn_rate, clip_scale)
            return new_w, new_m, new_v, new_w.astype(BF16)

        return tuple(a.T for a in lax.cond(flag, slow, fast, None))

    return jax.shard_map(local_step, mesh=mesh, in_specs=(row_spec, act_spec, table_spec, table_spec, table_spec, table_spec, P(), P()), out_specs=(table_spec, table_spec, table_spec, table_spec), check_vma=False)
```

profile of v0, /device:TPU:0, one launch (start us, length us, event | category | flops | bytes accessed | tf_op | source)
XLA Modules:
  0.0 103.4 jit_solution(6175802291955470548)
XLA Ops:
  1.9 0.1 pad_maximum_fusion
  2.0 0.7 copy.13
  2.7 93.5 %assemble.1 = f32[64,16,256]{2,1,0:T(8,128)S(1)} custom-call(s32[1,4096]{1,0:T(1,128)S(1)} %bitcast.30, bf16[4096,1024]{1,0:T(8,128)(2,1)} %bitcast.20), custom_call_target="tpu_custom_call" | custom-call | tf_op jit(solution)/shard_map/assemble/pallas_call | solution.py:370
  96.2 0.7 slice_reduce_fusion
  97.6 5.8 %conditional.1 = ((f32[16,16064]{1,0:T(8,128)}, f32[16,16064]{1,0:T(8,128)}, f32[16,16064]{1,0:T(8,128)}, bf16[16,16064]{1,0:T(8,128)(2,1)})) conditional(s32[]{:T(128)} %convert_element_type.6, (f32[2]{0:T(128)S(1)}, f32[64,16,256]{2,1,0:T(8,128)S(1)}, f32[16,16064]{1,0:T(8,128)}, f32[16,16064]{1,0:T(8,128)}, f32[16,16064]{1,0:T(8,128)}, ...), branch_computations={%region_1.0_spmd, %region_2.0_spmd} | conditional | flops 20308996 | bytes 549046528 | solution.py:410
  97.6 5.8 %finish.1 = (f32[16,16064]{1,0:T(8,128)}, f32[16,16064]{1,0:T(8,128)}, f32[16,16064]{1,0:T(8,128)}, bf16[16,16064]{1,0:T(8,128)(2,1)}) custom-call(f32[2]{0:T(128)S(1)} %get-tuple-element.28.scal_ref, f32[64,16,256]{2,1,0:T(8,128)S(1)} %get-tuple-element.29.recv_ref, f32[16,16064]{1,0:T(8,128)} %get-tuple-element.30.head_ref, ...), custom_call_target="tpu_custom_call" | custom-call | tf_op jit(solution)/shard_map/cond/branch_0_fun/finish/pallas_call | solution.py:395
where the time goes:
time: 105 us; the launch traced here: 103 us
  Pallas kernels  99.3 us (95%)
  between operations  2.59 us (2%)
    pallas_call x1, Pallas kernels, local_step(): pl.pallas_call(assemble, out_shape=shaped(64, 16, 256), in_specs=[pl.Bloc...  93.5 us
    pallas_call x1, Pallas kernels, fast(): pl.pallas_call(finish, out_shape=(shaped(*shard), shaped(*shard), shaped(...  5.79 us

commit v1 on v0

v1 whole, which is shorter than its diff:
```python
import functools

import jax
import jax.numpy as jnp
from jax import lax
from jax.experimental import pallas as pl
from jax.experimental.pallas import tpu as pltpu
from jax.sharding import PartitionSpec as P

OPT_STEP = 20
F32, BF16, I32, I16 = jnp.float32, jnp.bfloat16, jnp.int32, jnp.int16
CAP = (480, 352, 208)
KW = 512
STRIDES = ((1, 16), (4, 1), (16, 4))
VLIM = 20 << 20
MESH = pl.DeviceIdType.MESH
CHUNK = 256


def update_math(embed_grad, head_grad, master_w, moment_m, moment_v, learn_rate, clip_scale):
    beta_two = 1.0 - OPT_STEP ** -0.8
    grad_full = clip_scale * (embed_grad + head_grad)
    new_v = beta_two * moment_v + (1.0 - beta_two) * (grad_full * grad_full + 1e-30)
    new_m = 0.9 * moment_m + 0.1 * (grad_full / jnp.sqrt(new_v))
    new_w = master_w - learn_rate * new_m - learn_rate * learn_rate * master_w
    return new_w, new_m, new_v


def iota(shape, dim):
    return lax.broadcasted_iota(I32, shape, dim)


def onehot(cond):
    return jnp.where(cond, 1.0, 0.0).astype(BF16)


def slots_hot(slots, first, cap):
    row = (slots - first).astype(I16)
    return jnp.where(lax.broadcasted_iota(I16, (cap, slots.shape[1]), 0) == row, BF16(1), BF16(0))


def dot_nt(a, b):
    return lax.dot_general(a, b, (((1,), (1,)), ((), ())), preferred_element_type=F32)


def dot_nn(a, b):
    return jnp.dot(a, b, preferred_element_type=F32)


def ranks(pres, group):
    rows = pres.shape[0]
    pres_b = pres.astype(BF16)
    before = onehot(iota((KW, KW), 0) < iota((KW, KW), 1))
    inner = dot_nn(pres_b, before)
    if group > 1:
        r, c = iota((rows, rows), 0), iota((rows, rows), 1)
        above = onehot((c < r) & (c // group == r // group))
        inner = inner + jnp.sum(dot_nn(above, pres_b), axis=1, keepdims=True)
    return inner.astype(I32)


def codes(pres, group, cap):
    rows = pres.shape[0]
    rank = ranks(pres, group)
    code = jnp.where((pres > 0.5) & (rank < cap), (iota((rows, KW), 0) // group) * cap + rank + 1, 0)
    over = jnp.where((pres > 0.5) & (rank >= cap), 1.0, 0.0)
    return code, jnp.max(over)


def index_first(coords, tok_ref, slot_ref, tables):
    ids = jnp.concatenate([tok_ref[r:r + 1] for r in range(tok_ref.shape[0])], axis=1)
    tp, c1, c2, c3 = coords
    x, y, z = ids & 3, (ids >> 2) & 3, (ids >> 4) & 3
    d1 = x + (z - x) * tp
    d2 = y + (x - y) * tp
    d3 = z + (y - z) * tp
    q = (((d1 - c1) & 3) << 4) + (((d2 - c2) & 3) << 2) + ((d3 - c3) & 3)
    upper = ids >= 16064
    kk = jnp.where(upper, ids - 16064, ids) >> 6
    k = jnp.where(upper, 256, 0) + ((kk & 1) << 7) + (kk >> 1)
    n = ids.shape[1]
    hot_q = onehot(iota((64, n), 0) == q)
    hot_k = onehot(iota((KW, n), 0) == k)
    pres = jnp.minimum(dot_nt(hot_q, hot_k), 1.0)
    code, over = codes(pres, 16, CAP[0])
    both = jnp.concatenate([(code >> 5).astype(BF16), (code & 31).astype(BF16)], axis=0)
    found = dot_nn(both, hot_k)
    value = found[:64] * 32.0 + found[64:]
    slot_ref[...] = jnp.sum(jnp.where(iota((64, n), 0) == q, value, 0.0), axis=0, keepdims=True).astype(I32) - 1
    for o in range(4):
        tables[o] = pres[16 * o:16 * o + 16]
    return over


def gather_first(o, slot_ref, rows_ref, outs):
    cap, depth = outs[0].shape[0], 1024

    def step(n, first):
        at = pl.ds(pl.multiple_of(n * depth, depth), depth)
        part = dot_nn(slots_hot(slot_ref[:, at], o * cap, cap), rows_ref[at, :])
        for chunk, out in enumerate(outs):
            piece = part[:, CHUNK * chunk:CHUNK * chunk + CHUNK]
            out[...] = piece if first else out[...] + piece

    step(0, True)
    lax.fori_loop(1, rows_ref.shape[0] // depth, lambda n, c: (step(n, False), c)[1], 0)


def index_next(group, cap_in, cap_out, blocks, slot_ref, tables):
    rows = 4 * group
    blocks = [block[:rows] for block in blocks]
    merged = jnp.minimum(blocks[0] + blocks[1] + blocks[2] + blocks[3], 1.0)
    code, over = codes(merged, group, cap_out)
    hi, lo = (code >> 5).astype(F32), (code & 31).astype(F32)
    every = jnp.concatenate(blocks, axis=0)
    every = jnp.where(every > 0.5, ranks(every, rows), -1)
    spread = onehot((iota((16, KW), 1) >> 5) == iota((16, KW), 0))
    own_row = (iota((32, KW), 1) & 31) == iota((32, KW), 0)
    found = []
    for s in range(4):
        highs, lows = [], []
        for r in range(rows):
            row = every[rows * s + r:rows * s + r + 1]
            highs.append(onehot(iota((16, KW), 0) == (row >> 5)))
            low = iota((32, KW), 0) == (row & 31)
            low = jnp.concatenate([jnp.where(low, hi[r:r + 1], 0.0), jnp.where(low, lo[r:r + 1], 0.0)], axis=0)
            lows.append(low.astype(BF16))
        table = dot_nt(jnp.concatenate(lows, axis=1), jnp.concatenate(highs, axis=1)).astype(BF16)
        value = dot_nn(table, spread)
        value = jnp.where(own_row, value[:32] * 32.0 + value[32:], 0.0)
        found.append(jnp.sum(value, axis=0, keepdims=True)[:, :cap_in])
    slot_ref[:, :4 * cap_in] = jnp.concatenate(found, axis=1).astype(I32) - 1
    tables[...] = jnp.zeros(tables.shape, F32)
    for o in range(4):
        tables[o, :group] = merged[group * o:group * o + group]
    return over


def split_rows(rows):
    high = jnp.clip(rows, -3.38e38, 3.38e38).astype(BF16)
    rest = rows - high.astype(F32)
    mid = rest.astype(BF16)
    return high, mid, (rest - mid.astype(F32)).astype(BF16)


def split_blocks(blocks, pieces):
    cap = blocks[0].shape[0]
    for s, rows in enumerate(blocks):
        for n, piece in enumerate(split_rows(rows[...])):
            pieces[n, cap * s:cap * s + cap] = piece


def gather_next(o, depth, slot_ref, pieces, out_ref):
    cap = out_ref.shape[0]
    hot = slots_hot(slot_ref[:, :depth], o * cap, cap)
    out_ref[...] = dot_nn(hot, pieces[0, :depth]) + dot_nn(hot, pieces[1, :depth]) + dot_nn(hot, pieces[2, :depth])


def dense_last(tables, blocks, flag, out_ref):
    pres = jnp.concatenate([table[...] for table in tables], axis=0)
    rank = jnp.where(pres > 0.5, ranks(pres, 1), -1)
    cap = blocks[0].shape[0]
    hot = jnp.concatenate([slots_hot(rank[8 * s:8 * s + 1], 0, cap) for s in range(4)], axis=0)
    rows = jnp.concatenate([block[...] for block in blocks], axis=0).T
    high, mid, low = split_rows(rows)
    total = dot_nn(high, hot) + dot_nn(mid, hot) + dot_nn(low, hot)
    total = jnp.where((iota(total.shape, 1) & 255) == 255, flag, total)
    for t in range(2):
        out_ref[t] = total[:, 256 * t:256 * t + 256].reshape(out_ref.shape[1:])


def assemble(tok_ref, rows_ref, recv_ref, half, slot1, slot2, slot3, tab1, tab2, tab3, rtab1, rtab2, rtab3, send1, send2, send3,
             recv1, recv2, recv3, pieces, own_over, peer_over, dense, half_sem, tab_out, tab_in, row_out, row_in, over_out, over_in, last_out, last_in):
    tp, me = lax.axis_index("tp"), lax.axis_index("fsdp")
    ring = []
    for low, high in STRIDES:
        stride = low + (high - low) * tp
        ring.append((stride, (me // stride) % 4))
    coords = (tp, *(at for _, at in ring))
    width = half.shape[1]
    same = 1 - (me // 32 + tp) % 2

    def neighbour(phase, offset):
        stride, at = ring[phase]
        return {"fsdp": me + stride * ((at + offset) % 4 - at)}

    barrier = pltpu.get_barrier_semaphore()

    def greet(device):
        pl.semaphore_signal(barrier, inc=1, device_id=device, device_id_type=MESH)

    for phase in range(3):
        for o in (1, 2, 3):
            greet(neighbour(phase, o))
    greet({"tp": 1 - tp})

    load = pltpu.make_async_copy(rows_ref.at[:, pl.ds(pl.multiple_of(tp * width, width), width)], half, half_sem)
    load.start()
    over = index_first(coords, tok_ref, slot1, tab1)
    pl.semaphore_wait(barrier, 10)

    def copy_to(src, dst, out, into, device):
        return pltpu.make_async_remote_copy(
            src_ref=src, dst_ref=dst, send_sem=out, recv_sem=into, device_id=device, device_id_type=MESH)

    def remote(*args):
        copy = copy_to(*args)
        copy.start()
        return copy

    def send_tables(phase, table, into):
        return [remote(table.at[o], into.at[o - 1], tab_out.at[3 * phase + o - 1], tab_in.at[3 * phase + o - 1], neighbour(phase, o))
                for o in (1, 2, 3)]

    def send_row(phase, chunk, o, rows, into):
        sem = 6 * phase + 3 * chunk + o - 1
        return copy_to(rows.at[chunk, o], into.at[chunk, o - 1], row_out.at[sem], row_in.at[sem], neighbour(phase, o))

    def wait(copies):
        for copy in copies:
            copy.wait()

    def beside(own, got):
        return [own.at[0], *(got.at[n] for n in range(3))]

    def loop_bins(step):
        lax.fori_loop(0, 3, lambda n, c: (step(2 - n + 3 * (n // 2)), c)[1], 0)

    def first(o):
        gather_first(o, slot1, half, [send1.at[chunk, o] for chunk in range(2)])

    def first_sent(o):
        first(o)
        send_row(0, 0, o, send1, recv1).start()

    def later(phase, chunk):
        slot, own, got, out, into = ((slot2, send1, recv1, send2, recv2), (slot3, send2, recv2, send3, recv3))[phase - 1]
        blocks = beside(own.at[chunk], got.at[chunk])
        depth = 4 * CAP[phase - 1]
        split_blocks(blocks, pieces)

        def sent(o):
            gather_next(o, depth, slot, pieces, out.at[chunk, o])
            send_row(phase, chunk, o, out, into).start()

        loop_bins(sent)
        gather_next(0, depth, slot, pieces, out.at[chunk, 0])

    def wait_rows(phase, chunk):
        out, into = ((send1, recv1), (send2, recv2), (send3, recv3))[phase]
        for o in (1, 2, 3):
            send_row(phase, chunk, o, out, into).wait()

    def finish_chunk(chunk):
        dense_last(beside(tab3, rtab3), beside(send3.at[chunk], recv3.at[chunk]), flag, dense.at[chunk])

    tables1 = send_tables(0, tab1, rtab1)
    load.wait()
    loop_bins(first_sent)
    for o in (2, 1, 3):
        send_row(0, 1, o, send1, recv1).start()
    wait(tables1)
    over = jnp.maximum(over, index_next(4, CAP[0], CAP[1], beside(tab1, rtab1), slot2, tab2))
    tables2 = send_tables(1, tab2, rtab2)
    first(0)
    wait(tables2)
    over = jnp.maximum(over, index_next(1, CAP[1], CAP[2], beside(tab2, rtab2), slot3, tab3))
    own_over[...] = jnp.full(own_over.shape, over, F32)
    tables3 = send_tables(2, tab3, rtab3)
    tables3.append(remote(own_over, peer_over, over_out, over_in, {"tp": 1 - tp}))
    wait_rows(0, 0)

    @pl.when(tp == 1)
    def _():
        wait_rows(0, 1)

    later(1, 0)

    @pl.when(tp == 0)
    def _():
        wait_rows(0, 1)

    later(1, 1)
    wait_rows(1, 0)
    later(2, 0)
    wait(tables3)
    flag = jnp.maximum(own_over[0:1, 0:1], peer_over[0:1, 0:1])
    wait_rows(1, 1)
    later(2, 1)
    wait_rows(2, 0)
    finish_chunk(0)

    def last(i, far):
        at = (me + i) % 32
        core = (tp + far) % 2
        return pltpu.make_async_remote_copy(
            src_ref=dense.at[at // 16, core, at % 16], dst_ref=recv_ref.at[me], send_sem=last_out.at[2 * i + far],
            recv_sem=last_in.at[me], device_id={"fsdp": 32 * tp + at, "tp": core}, device_id_type=MESH)

    def arrive(j):
        return pltpu.make_async_remote_copy(
            src_ref=dense.at[0, 0, 0], dst_ref=recv_ref.at[j], send_sem=last_out.at[0], recv_sem=last_in.at[j],
            device_id={"tp": 1 - tp}, device_id_type=MESH)

    def each_pair(chunk, act, self_act):
        def pair(n, carry):
            at = 16 * chunk + (me + n) % 16
            i = (at - me % 32 + 32) % 32
            act(last(i, 1))

            @pl.when((same == 0) | (i > 0))
            def _():
                act(last(i, 0))

            @pl.when((same == 1) & (i == 0))
            def _():
                self_act()

            return carry

        lax.fori_loop(0, 16, pair, 0)

    def keep():
        recv_ref[me] = dense[(me % 32) // 16, tp, me % 16]

    each_pair(0, lambda copy: copy.start(), keep)
    wait_rows(2, 1)
    finish_chunk(1)
    each_pair(1, lambda copy: copy.start(), keep)

    def wait_arrival(i, carry):
        arrive((me + i) % 64).wait_recv()
        return carry

    lax.fori_loop(1, 64, wait_arrival, 0)

    @pl.when(same == 0)
    def _():
        arrive(me).wait_recv()

    each_pair(0, lambda copy: copy.wait_send(), lambda: None)
    each_pair(1, lambda copy: copy.wait_send(), lambda: None)


def finish(scal_ref, recv_ref, head_ref, w_ref, m_ref, v_ref, w_out, m_out, v_out, b_out, grad):
    tiles = grad.shape[0]
    for c in range(16):
        both = jnp.concatenate([recv_ref[:, c, :128], recv_ref[:, c, 128:]], axis=0)
        grad[:, c, :] = both.T[:tiles]
    lr, clip = scal_ref[0], scal_ref[1]
    rows = head_ref.shape[1]
    for t in range(tiles):
        at = slice(128 * t, min(128 * t + 128, rows))
        width = at.stop - at.start
        new_w, new_m, new_v = update_math(grad[t, :, :width], head_ref[:, at], w_ref[:, at], m_ref[:, at], v_ref[:, at], lr, clip)
        w_out[:, at], m_out[:, at], v_out[:, at] = new_w, new_m, new_v
        b_out[:, at] = new_w.astype(BF16)


def shaped(*shape, dtype=F32):
    return jax.ShapeDtypeStruct(shape, dtype)


def dense_rows(ids_ref, rows_ref, out_ref):
    first = pl.program_id(0) * out_ref.shape[0]
    hot = onehot(iota((out_ref.shape[0], rows_ref.shape[0]), 0) + first == ids_ref[...])
    part = dot_nn(hot, rows_ref[...])

    @pl.when(pl.program_id(1) == 0)
    def _():
        out_ref[...] = part

    @pl.when(pl.program_id(1) > 0)
    def _():
        out_ref[...] += part


def solution(mesh):
    row_spec = P(("dp", "fsdp"), None)
    act_spec = P(("dp", "fsdp"), None, None)
    table_spec = P(("dp", "tp"), "fsdp")

    def dense_grad(ids, rows, shard_rows):
        n, width = rows.shape
        block, depth = 256, 1024
        tiles = -(-shard_rows // block)
        part = pl.pallas_call(
            dense_rows,
            grid=(tiles, n // depth),
            in_specs=[pl.BlockSpec((1, depth), lambda i, k: (0, k)), pl.BlockSpec((depth, width), lambda i, k: (k, 0))],
            out_specs=pl.BlockSpec((block, width), lambda i, k: (i, 0)),
            out_shape=shaped(tiles * block, width),
            compiler_params=pltpu.CompilerParams(vmem_limit_bytes=VLIM),
            name="dense_rows",
        )(ids - lax.axis_index("tp") * shard_rows, rows)
        part = part[:shard_rows].T.reshape(64, 16, shard_rows)
        return jnp.sum(lax.all_to_all(part, "fsdp", 0, 0, tiled=True), axis=0)

    def local_step(tokens, out_grad, head_grad, master_w, moment_m, moment_v, learn_rate, clip_scale):
        n = tokens.size
        rows = out_grad.reshape(n, -1)
        width = rows.shape[1] // 2
        vm, dma = pltpu.VMEM, pltpu.SemaphoreType.DMA
        recv = pl.pallas_call(
            assemble,
            out_shape=shaped(64, 16, 256),
            in_specs=[pl.BlockSpec(memory_space=vm), pl.BlockSpec(memory_space=pl.ANY)],
            out_specs=pl.BlockSpec(memory_space=vm),
            scratch_shapes=[
                vm((n, width), BF16), vm((1, n), I32), vm((1, 4 * KW), I32), vm((1, 4 * KW), I32),
                vm((4, 16, KW), F32), vm((4, 8, KW), F32), vm((4, 8, KW), F32),
                vm((3, 16, KW), F32), vm((3, 8, KW), F32), vm((3, 8, KW), F32),
                *[vm((2, 4, cap, CHUNK), F32) for cap in CAP],
                *[vm((2, 3, cap, CHUNK), F32) for cap in CAP],
                vm((3, 4 * CAP[0], CHUNK), BF16),
                vm((8, 128), F32), vm((8, 128), F32), vm((2, 2, 16, 16, 256), F32),
                dma, dma((9,)), dma((9,)), dma((18,)), dma((18,)), dma, dma, dma((64,)), dma((64,)),
            ],
            compiler_params=pltpu.CompilerParams(vmem_limit_bytes=40 << 20, collective_id=0, has_side_effects=True),
            name="assemble",
        )(tokens, rows)
        flag = jnp.max(recv[:, 0, 255]) > 0.5

        scal = jnp.stack([learn_rate, clip_scale])
        tables = (head_grad.T, master_w.T, moment_m.T, moment_v.T)
        shard_rows = master_w.shape[0]
        shard = (16, shard_rows)

        def fast(_):
            return pl.pallas_call(
                finish,
                out_shape=(shaped(*shard), shaped(*shard), shaped(*shard), shaped(*shard, dtype=BF16)),
                in_specs=[pl.BlockSpec(memory_space=pltpu.SMEM)] + [pl.BlockSpec(memory_space=pltpu.VMEM)] * 5,
                out_specs=tuple(pl.BlockSpec(memory_space=pltpu.VMEM) for _ in range(4)),
                scratch_shapes=[pltpu.VMEM(((shard_rows + 127) // 128, 16, 128), F32)],
                compiler_params=pltpu.CompilerParams(vmem_limit_bytes=VLIM),
                name="finish",
            )(scal, recv, *tables)

        def slow(_):
            grad = dense_grad(tokens.reshape(1, -1), rows, shard_rows)
            new_w, new_m, new_v = update_math(grad, *tables, learn_rate, clip_scale)
            return new_w, new_m, new_v, new_w.astype(BF16)

        return tuple(a.T for a in lax.cond(flag, slow, fast, None))

    return jax.shard_map(local_step, mesh=mesh, in_specs=(row_spec, act_spec, table_spec, table_spec, table_spec, table_spec, P(), P()), out_specs=(table_spec, table_spec, table_spec, table_spec), check_vma=False)
```

time: 105 us -> 89.4 us (0.85)
  the two profiles are of different devices: /device:TPU:0 before, /device:TPU:97 now
where the time goes in v1:
time: 89.4 us; the launch traced here: 89.2 us
  Pallas kernels  85.8 us (96%)
  between operations  2.59 us (3%)
    pallas_call x1, Pallas kernels, local_step(): pl.pallas_call(assemble, out_shape=shaped(64, 16, 256), in_specs=[pl.Bloc...  80 us
    pallas_call x1, Pallas kernels, fast(): pl.pallas_call(finish, out_shape=(shaped(*shard), shaped(*shard), shaped(...  5.79 us

profile of v1, /device:TPU:97, one launch (start us, length us, event | category | flops | bytes accessed | tf_op | source)
XLA Modules:
  0.0 89.2 jit_solution(5704519085360655522)
XLA Ops:
  1.9 0.1 pad_maximum_fusion
  2.0 80.0 %assemble.1 = f32[64,16,256]{2,1,0:T(8,128)S(1)} custom-call(s32[2,2048]{1,0:T(2,128)} %tok_ref.1, bf16[4096,1024]{1,0:T(8,128)(2,1)} %bitcast.22), custom_call_target="tpu_custom_call" | custom-call | tf_op jit(solution)/shard_map/assemble/pallas_call | solution.py:404
  82.0 0.7 slice_reduce_fusion
  83.4 5.8 %conditional.1 = ((f32[16,16064]{1,0:T(8,128)}, f32[16,16064]{1,0:T(8,128)}, f32[16,16064]{1,0:T(8,128)}, bf16[16,16064]{1,0:T(8,128)(2,1)})) conditional(s32[]{:T(128)} %convert_element_type.6, (f32[2]{0:T(128)S(1)}, f32[64,16,256]{2,1,0:T(8,128)S(1)}, f32[16,16064]{1,0:T(8,128)}, f32[16,16064]{1,0:T(8,128)}, f32[16,16064]{1,0:T(8,128)}, ...), branch_computations={%region_1.0_spmd, %region_2.0_spmd} | conditional | flops 20308996 | bytes 549079296 | solution.py:445
  83.4 5.8 %finish.1 = (f32[16,16064]{1,0:T(8,128)}, f32[16,16064]{1,0:T(8,128)}, f32[16,16064]{1,0:T(8,128)}, bf16[16,16064]{1,0:T(8,128)(2,1)}) custom-call(f32[2]{0:T(128)S(1)} %get-tuple-element.28.scal_ref, f32[64,16,256]{2,1,0:T(8,128)S(1)} %get-tuple-element.29.recv_ref, f32[16,16064]{1,0:T(8,128)} %get-tuple-element.30.head_ref, ...), custom_call_target="tpu_custom_call" | custom-call | tf_op jit(solution)/shard_map/cond/branch_0_fun/finish/pallas_call | solution.py:430

commit v2 on v1

--- a/solution.py
+++ b/solution.py
@@ -92,12 +92,13 @@
     return over
 
 
-def gather_first(o, slot_ref, rows_ref, outs):
+def gather_first(o, slot_ref, rows_ref, outs, start):
     cap, depth = outs[0].shape[0], 1024
+    columns = pl.ds(start, CHUNK * len(outs))
 
     def step(n, first):
         at = pl.ds(pl.multiple_of(n * depth, depth), depth)
-        part = dot_nn(slots_hot(slot_ref[:, at], o * cap, cap), rows_ref[at, :])
+        part = dot_nn(slots_hot(slot_ref[:, at], o * cap, cap), rows_ref[at, columns])
         for chunk, out in enumerate(outs):
             piece = part[:, CHUNK * chunk:CHUNK * chunk + CHUNK]
             out[...] = piece if first else out[...] + piece
@@ -169,8 +170,8 @@
         out_ref[t] = total[:, 256 * t:256 * t + 256].reshape(out_ref.shape[1:])
 
 
-def assemble(tok_ref, rows_ref, recv_ref, half, slot1, slot2, slot3, tab1, tab2, tab3, rtab1, rtab2, rtab3, send1, send2, send3,
-             recv1, recv2, recv3, pieces, own_over, peer_over, dense, half_sem, tab_out, tab_in, row_out, row_in, over_out, over_in, last_out, last_in):
+def assemble(tok_ref, rows_ref, head_ref, w_ref, m_ref, v_ref, recv_ref, head_out, w_out, m_out, v_out, half, slot1, slot2, slot3, tab1, tab2, tab3, rtab1, rtab2, rtab3, send1, send2, send3,
+             recv1, recv2, recv3, pieces, own_over, peer_over, dense, table_sem, half_sem, tab_out, tab_in, row_out, row_in, over_out, over_in, last_out, last_in):
     tp, me = lax.axis_index("tp"), lax.axis_index("fsdp")
     ring = []
     for low, high in STRIDES:
@@ -198,6 +199,8 @@
     load.start()
     over = index_first(coords, tok_ref, slot1, tab1)
     pl.semaphore_wait(barrier, 10)
+    loads = [pltpu.make_async_copy(src, dst, table_sem.at[n])
+             for n, (src, dst) in enumerate(((head_ref, head_out), (w_ref, w_out), (m_ref, m_out), (v_ref, v_out)))]
 
     def copy_to(src, dst, out, into, device):
         return pltpu.make_async_remote_copy(
@@ -226,14 +229,20 @@
     def loop_bins(step):
         lax.fori_loop(0, 3, lambda n, c: (step(2 - n + 3 * (n // 2)), c)[1], 0)
 
-    def first(o):
-        gather_first(o, slot1, half, [send1.at[chunk, o] for chunk in range(2)])
-
-    def first_sent(o):
-        first(o)
-        send_row(0, 0, o, send1, recv1).start()
-
-    def later(phase, chunk):
+    def first(*chunks):
+        def step(o):
+            gather_first(o, slot1, half, [send1.at[chunk, o] for chunk in chunks], CHUNK * chunks[0])
+
+        return step
+
+    def first_sent(chunk):
+        def step(o):
+            first(chunk)(o)
+            send_row(0, chunk, o, send1, recv1).start()
+
+        return step
+
+    def later(phase, chunk, hold=False):
         slot, own, got, out, into = ((slot2, send1, recv1, send2, recv2), (slot3, send2, recv2, send3, recv3))[phase - 1]
         blocks = beside(own.at[chunk], got.at[chunk])
         depth = 4 * CAP[phase - 1]
@@ -241,9 +250,19 @@
 
         def sent(o):
             gather_next(o, depth, slot, pieces, out.at[chunk, o])
-            send_row(phase, chunk, o, out, into).start()
+            if hold:
+                pl.when(tp == 0)(send_row(phase, chunk, o, out, into).start)
+            else:
+                send_row(phase, chunk, o, out, into).start()
 
         loop_bins(sent)
+        if hold:
+            @pl.when(tp == 1)
+            def _():
+                wait_rows(0, 1)
+                for o in (2, 1, 3):
+                    send_row(phase, chunk, o, out, into).start()
+
         gather_next(0, depth, slot, pieces, out.at[chunk, 0])
 
     def wait_rows(phase, chunk):
@@ -256,13 +275,14 @@
 
     tables1 = send_tables(0, tab1, rtab1)
     load.wait()
-    loop_bins(first_sent)
-    for o in (2, 1, 3):
-        send_row(0, 1, o, send1, recv1).start()
+    loop_bins(first_sent(0))
+    loop_bins(first_sent(1))
+    for table in loads:
+        table.start()
     wait(tables1)
     over = jnp.maximum(over, index_next(4, CAP[0], CAP[1], beside(tab1, rtab1), slot2, tab2))
     tables2 = send_tables(1, tab2, rtab2)
-    first(0)
+    first(0, 1)(0)
     wait(tables2)
     over = jnp.maximum(over, index_next(1, CAP[1], CAP[2], beside(tab2, rtab2), slot3, tab3))
     own_over[...] = jnp.full(own_over.shape, over, F32)
@@ -270,11 +290,7 @@
     tables3.append(remote(own_over, peer_over, over_out, over_in, {"tp": 1 - tp}))
     wait_rows(0, 0)
 
-    @pl.when(tp == 1)
-    def _():
-        wait_rows(0, 1)
-
-    later(1, 0)
+    later(1, 0, hold=True)
 
     @pl.when(tp == 0)
     def _():
@@ -304,7 +320,7 @@
 
     def each_pair(chunk, act, self_act):
         def pair(n, carry):
-            at = 16 * chunk + (me + n) % 16
+            at = 16 * chunk + (7 * me + 5 * (me // 16) + n) % 16
             i = (at - me % 32 + 32) % 32
             act(last(i, 1))
 
@@ -338,16 +354,17 @@
     def _():
         arrive(me).wait_recv()
 
+    wait(loads)
     each_pair(0, lambda copy: copy.wait_send(), lambda: None)
     each_pair(1, lambda copy: copy.wait_send(), lambda: None)
 
 
-def finish(scal_ref, recv_ref, head_ref, w_ref, m_ref, v_ref, w_out, m_out, v_out, b_out, grad):
+def finish(lr_ref, clip_ref, recv_ref, head_ref, w_ref, m_ref, v_ref, w_out, m_out, v_out, b_out, grad):
     tiles = grad.shape[0]
     for c in range(16):
         both = jnp.concatenate([recv_ref[:, c, :128], recv_ref[:, c, 128:]], axis=0)
         grad[:, c, :] = both.T[:tiles]
-    lr, clip = scal_ref[0], scal_ref[1]
+    lr, clip = lr_ref[0, 0], clip_ref[0, 0]
     rows = head_ref.shape[1]
     for t in range(tiles):
         at = slice(128 * t, min(128 * t + 128, rows))
@@ -401,11 +418,14 @@
         rows = out_grad.reshape(n, -1)
         width = rows.shape[1] // 2
         vm, dma = pltpu.VMEM, pltpu.SemaphoreType.DMA
-        recv = pl.pallas_call(
+        tables = (head_grad.T, master_w.T, moment_m.T, moment_v.T)
+        shard_rows = master_w.shape[0]
+        shard = (16, shard_rows)
+        recv, *near = pl.pallas_call(
             assemble,
-            out_shape=shaped(64, 16, 256),
-            in_specs=[pl.BlockSpec(memory_space=vm), pl.BlockSpec(memory_space=pl.ANY)],
-            out_specs=pl.BlockSpec(memory_space=vm),
+            out_shape=(shaped(64, 16, 256), *[shaped(*shard)] * 4),
+            in_specs=[pl.BlockSpec(memory_space=vm)] + [pl.BlockSpec(memory_space=pl.ANY)] * 5,
+            out_specs=tuple([pl.BlockSpec(memory_space=vm)] * 5),
             scratch_shapes=[
                 vm((n, width), BF16), vm((1, n), I32), vm((1, 4 * KW), I32), vm((1, 4 * KW), I32),
                 vm((4, 16, KW), F32), vm((4, 8, KW), F32), vm((4, 8, KW), F32),
@@ -414,28 +434,24 @@
                 *[vm((2, 3, cap, CHUNK), F32) for cap in CAP],
                 vm((3, 4 * CAP[0], CHUNK), BF16),
                 vm((8, 128), F32), vm((8, 128), F32), vm((2, 2, 16, 16, 256), F32),
-                dma, dma((9,)), dma((9,)), dma((18,)), dma((18,)), dma, dma, dma((64,)), dma((64,)),
+                dma((4,)), dma, dma((9,)), dma((9,)), dma((18,)), dma((18,)), dma, dma, dma((64,)), dma((64,)),
             ],
             compiler_params=pltpu.CompilerParams(vmem_limit_bytes=40 << 20, collective_id=0, has_side_effects=True),
             name="assemble",
-        )(tokens, rows)
+        )(tokens, rows, *tables)
         flag = jnp.max(recv[:, 0, 255]) > 0.5
 
-        scal = jnp.stack([learn_rate, clip_scale])
-        tables = (head_grad.T, master_w.T, moment_m.T, moment_v.T)
-        shard_rows = master_w.shape[0]
-        shard = (16, shard_rows)
-
         def fast(_):
+            vm, scalar = pl.BlockSpec(memory_space=pltpu.VMEM), pl.BlockSpec(memory_space=pltpu.SMEM)
             return pl.pallas_call(
                 finish,
                 out_shape=(shaped(*shard), shaped(*shard), shaped(*shard), shaped(*shard, dtype=BF16)),
-                in_specs=[pl.BlockSpec(memory_space=pltpu.SMEM)] + [pl.BlockSpec(memory_space=pltpu.VMEM)] * 5,
-                out_specs=tuple(pl.BlockSpec(memory_space=pltpu.VMEM) for _ in range(4)),
+                in_specs=[scalar, scalar, vm, vm, vm, vm, vm],
+                out_specs=(vm, vm, vm, vm),
                 scratch_shapes=[pltpu.VMEM(((shard_rows + 127) // 128, 16, 128), F32)],
                 compiler_params=pltpu.CompilerParams(vmem_limit_bytes=VLIM),
                 name="finish",
-            )(scal, recv, *tables)
+            )(learn_rate.reshape(1, 1), clip_scale.reshape(1, 1), recv, *near)
 
         def slow(_):
             grad = dense_grad(tokens.reshape(1, -1), rows, shard_rows)

time: 89.4 us -> 88.5 us (0.990)
  the two profiles are of different devices: /device:TPU:97 before, /device:TPU:38 now
where the time goes in v2:
time: 88.5 us; the launch traced here: 88.3 us
  Pallas kernels  86.2 us (97%)
  between operations  1.29 us (1%)
    pallas_call x1, Pallas kernels, local_step(): pl.pallas_call(assemble, out_shape=(shaped(64, 16, 256), *[shaped(*shard)...  79.8 us
    pallas_call x1, Pallas kernels, fast(): pl.pallas_call(finish, out_shape=(shaped(*shard), shaped(*shard), shaped(...  6.45 us

profile of v2, /device:TPU:38, one launch (start us, length us, event | category | flops | bytes accessed | tf_op | source)
XLA Modules:
  0.0 88.3 jit_solution(5625709356565933405)
XLA Ops:
  0.6 79.8 %assemble.1 = (f32[64,16,256]{2,1,0:T(8,128)S(1)}, f32[16,16064]{1,0:T(8,128)S(1)}, f32[16,16064]{1,0:T(8,128)S(1)}, f32[16,16064]{1,0:T(8,128)}, f32[16,16064]{1,0:T(8,128)}) custom-call(s32[2,2048]{1,0:T(2,128)} %tok_ref.1, bf16[4096,1024]{1,0:T(8,128)(2,1)} %bitcast.20, f32[16,16064]{1,0:T(8,128)} %bitcast.22, f32[16,16064]{1,0:T(8,128)} %bitcast.24, ...), custom_call_target="tpu_custom_call" | custom-call | tf_op jit(solution)/shard_map/assemble/pallas_call | solution.py:424
  80.4 0.7 slice_reduce_fusion
  81.8 6.5 %conditional.1 = ((f32[16,16064]{1,0:T(8,128)}, f32[16,16064]{1,0:T(8,128)}, f32[16,16064]{1,0:T(8,128)}, bf16[16,16064]{1,0:T(8,128)(2,1)})) conditional(s32[]{:T(128)} %convert_element_type.6, (f32[]{:T(128)}, f32[]{:T(128)}, f32[64,16,256]{2,1,0:T(8,128)S(1)}, f32[16,16064]{1,0:T(8,128)S(1)}, f32[16,16064]{1,0:T(8,128)S(1)}, ...), branch_computations={%region_1.0_spmd, %region_2.0_spmd} | conditional | flops 20308996 | bytes 549079296 | solution.py:461
  81.8 6.5 %finish.1 = (f32[16,16064]{1,0:T(8,128)}, f32[16,16064]{1,0:T(8,128)}, f32[16,16064]{1,0:T(8,128)}, bf16[16,16064]{1,0:T(8,128)(2,1)}) custom-call(f32[1,1]{1,0:T(1,128)} %bitcast.lr_ref, f32[1,1]{1,0:T(1,128)} %bitcast.1.clip_ref, f32[64,16,256]{2,1,0:T(8,128)S(1)} %get-tuple-element.32.recv_ref, f32[16,16064]{1,0:T(8,128)S(1)} %get-tuple-element.33.head_ref, ...), custom_call_target="tpu_custom_call" | custom-call | tf_op jit(solution)/shard_map/cond/branch_0_fun/finish/pallas_call | solution.py:446

commit v3 on v2

--- a/solution.py
+++ b/solution.py
@@ -301,11 +301,6 @@
     later(2, 0)
     wait(tables3)
     flag = jnp.maximum(own_over[0:1, 0:1], peer_over[0:1, 0:1])
-    wait_rows(1, 1)
-    later(2, 1)
-    wait_rows(2, 0)
-    finish_chunk(0)
-
     def last(i, far):
         at = (me + i) % 32
         core = (tp + far) % 2
@@ -339,7 +334,21 @@
     def keep():
         recv_ref[me] = dense[(me % 32) // 16, tp, me % 16]
 
-    each_pair(0, lambda copy: copy.start(), keep)
+    @pl.when(tp == 0)
+    def _():
+        wait_rows(2, 0)
+        finish_chunk(0)
+        each_pair(0, lambda copy: copy.start(), keep)
+
+    wait_rows(1, 1)
+    later(2, 1)
+
+    @pl.when(tp == 1)
+    def _():
+        wait_rows(2, 0)
+        finish_chunk(0)
+        each_pair(0, lambda copy: copy.start(), keep)
+
     wait_rows(2, 1)
     finish_chunk(1)
     each_pair(1, lambda copy: copy.start(), keep)

time: 88.5 us -> 90.8 us (1.026)
  the two profiles are of different devices: /device:TPU:38 before, /device:TPU:50 now
where the time goes in v3:
time: 90.8 us; the launch traced here: 90.6 us
  Pallas kernels  88.5 us (97%)
  between operations  1.29 us (1%)
    pallas_call x1, Pallas kernels, local_step(): pl.pallas_call(assemble, out_shape=(shaped(64, 16, 256), *[shaped(*shard)...  82.1 us
    pallas_call x1, Pallas kernels, fast(): pl.pallas_call(finish, out_shape=(shaped(*shard), shaped(*shard), shaped(...  6.45 us

profile of v3, /device:TPU:50, one launch (start us, length us, event | category | flops | bytes accessed | tf_op | source)
XLA Modules:
  0.0 90.6 jit_solution(10955274374929967127)
XLA Ops:
  0.6 82.1 %assemble.1 = (f32[64,16,256]{2,1,0:T(8,128)S(1)}, f32[16,16064]{1,0:T(8,128)S(1)}, f32[16,16064]{1,0:T(8,128)S(1)}, f32[16,16064]{1,0:T(8,128)}, f32[16,16064]{1,0:T(8,128)}) custom-call(s32[2,2048]{1,0:T(2,128)} %tok_ref.1, bf16[4096,1024]{1,0:T(8,128)(2,1)} %bitcast.20, f32[16,16064]{1,0:T(8,128)} %bitcast.22, f32[16,16064]{1,0:T(8,128)} %bitcast.24, ...), custom_call_target="tpu_custom_call" | custom-call | tf_op jit(solution)/shard_map/assemble/pallas_call | solution.py:433
  82.7 0.7 slice_reduce_fusion
  84.1 6.5 %conditional.1 = ((f32[16,16064]{1,0:T(8,128)}, f32[16,16064]{1,0:T(8,128)}, f32[16,16064]{1,0:T(8,128)}, bf16[16,16064]{1,0:T(8,128)(2,1)})) conditional(s32[]{:T(128)} %convert_element_type.6, (f32[]{:T(128)}, f32[]{:T(128)}, f32[64,16,256]{2,1,0:T(8,128)S(1)}, f32[16,16064]{1,0:T(8,128)S(1)}, f32[16,16064]{1,0:T(8,128)S(1)}, ...), branch_computations={%region_1.0_spmd, %region_2.0_spmd} | conditional | flops 20308996 | bytes 549079296 | solution.py:470
  84.1 6.5 %finish.1 = (f32[16,16064]{1,0:T(8,128)}, f32[16,16064]{1,0:T(8,128)}, f32[16,16064]{1,0:T(8,128)}, bf16[16,16064]{1,0:T(8,128)(2,1)}) custom-call(f32[1,1]{1,0:T(1,128)} %bitcast.lr_ref, f32[1,1]{1,0:T(1,128)} %bitcast.1.clip_ref, f32[64,16,256]{2,1,0:T(8,128)S(1)} %get-tuple-element.32.recv_ref, f32[16,16064]{1,0:T(8,128)S(1)} %get-tuple-element.33.head_ref, ...), custom_call_target="tpu_custom_call" | custom-call | tf_op jit(solution)/shard_map/cond/branch_0_fun/finish/pallas_call | solution.py:455
